TPU v7x, 256 devices: a whole 4x4x8 slice. The times are simulated.
256 devices in a mesh: row: 16 (over y_lo, x, core), col: 16 (over z, y_hi).
Axes of the slice: x: 4, y: 4 (y_hi: 2, y_lo: 2; y = y_hi * 2 + y_lo), z: 8, core: 2. Of those that a mesh axis runs over, the one named last changes fastest.
Arguments:
- tokens: bfloat16 [2048, 8192], P('row', 'col'), may hold values from -200 to 200
- norm_gain: float32 [8192], P('col'), may hold values from 0.1 to 1.9
- gate_weight: bfloat16 [8192, 28672], P('col', 'row'), may hold values from -0.0625 to 0.0625
- up_weight: bfloat16 [8192, 28672], P('col', 'row'), may hold values from -0.0625 to 0.0625
- down_weight: bfloat16 [28672, 8192], P('row', 'col'), may hold values from -0.03125 to 0.03125
Outputs:
- mixed: bfloat16 [2048, 8192], P('row', 'col')
All inputs are finite; a program needn't handle non-finite values.
Results may differ from a plain program's by a relative error of at most 0.028.
Values may be sent and summed in bfloat16 or wider, within the bound.
A program may use at most 128 MiB of HBM per device.

v0:
```python
import jax
import jax.numpy as jnp
from jax import lax
from jax.sharding import Mesh
from jax.sharding import PartitionSpec as P

D = 8192
COL = ("col_0", "col_1")


def from_everyone(shard, axis):
    copies = jnp.broadcast_to(shard, (lax.axis_size(axis), *shard.shape))
    return lax.all_to_all(copies, axis, split_axis=0, concat_axis=0, tiled=True)


def taken_together(shard, axis):
    return from_everyone(shard, axis).sum(axis=0)


def in_order(blocks, dim):
    blocks = jnp.moveaxis(blocks, 0, dim)
    lengths = blocks.shape
    return blocks.reshape(*lengths[:dim], lengths[dim] * lengths[dim + 1], *lengths[dim + 2 :])


def gathered_copies(shard, axis, dim):
    blocks = from_everyone(shard, axis)
    return in_order(blocks, dim)


def own_rows(terms, axes):
    subtotal = terms.astype(jnp.bfloat16)
    for axis in axes:
        subtotal = lax.psum_scatter(subtotal, axis, scatter_dimension=0, tiled=True)
    return subtotal.astype(jnp.float32)


def gathered_by_axis(shard, axes, dim):
    for axis in reversed(axes):
        shard = lax.all_gather(shard, axis, axis=dim, tiled=True)
    return shard


def in_blocks(shard, dim, count):
    lengths = shard.shape
    blocks = shard.reshape(*lengths[:dim], count, lengths[dim] // count, *lengths[dim + 1 :])
    return jnp.moveaxis(blocks, dim, 0)


def sent_and_summed(shard, axis, dim):
    count = lax.axis_size(axis)
    blocks = lax.all_to_all(in_blocks(shard, dim, count), axis, 0, 0, tiled=True)
    return jnp.sum(blocks.astype(jnp.float32), axis=0)


def apply_norm(values, squares, norm_gain):
    scale = lax.rsqrt(squares / D + 1e-05)
    return (values.astype(jnp.float32) * scale[:, None] * norm_gain[None, :]).astype(jnp.bfloat16)


def body(tokens, norm_gain, gate_weight, up_weight, down_weight):
    own = tokens.astype(jnp.float32)
    squares = taken_together(jnp.sum(own * own, axis=1), COL)
    normed = apply_norm(tokens, squares, norm_gain)
    normed_all = gathered_copies(normed, "row", 0)
    hidden_width = gate_weight.shape[1]
    picked = normed_all
    gate_term = jnp.dot(picked, gate_weight, preferred_element_type=jnp.float32)
    up_term = jnp.dot(picked, up_weight, preferred_element_type=jnp.float32)
    sums = own_rows(jnp.concatenate([gate_term, up_term], axis=1), COL)
    hidden = (jax.nn.silu(sums[:, :hidden_width]) * sums[:, hidden_width:]).astype(jnp.bfloat16)
    hidden_all = gathered_by_axis(hidden, COL, 0)
    picked = hidden_all
    mixed = sent_and_summed(
        jnp.dot(picked, down_weight, preferred_element_type=jnp.float32).astype(jnp.bfloat16),
        "row",
        0,
    )
    return mixed.astype(jnp.bfloat16)


def solution(mesh):
    torus = Mesh(mesh.devices.reshape(mesh.shape["row"], 8, 2), ("row", "col_0", "col_1"))
    return jax.shard_map(
        body,
        mesh=torus,
        in_specs=(P("row", COL), P(COL), P(COL, "row"), P(COL, "row"), P("row", COL)),
        out_specs=P("row", COL),
        check_vma=False,
    )
```

profile of v0, /device:TPU:6, one launch (start us, length us, event | category | flops | bytes accessed | tf_op | source)
XLA Modules:
  0.0 424.7 jit_solution(2264880584324474611)
XLA Ops:
  6.5 0.0 copy-start
  6.5 0.0 reduce-scatter.5.cloned.1.call-start
  6.5 1.1 fusion.1
  7.7 21.0 %all_to_all.16 = f32[16,1,128]{2,1,0:T(1,128)S(1)} all-to-all(f32[16,1,128]{2,1,0:T(1,128)S(1)} %broadcast_in_dim.8), channel_id=1, replica_groups=mesh['row'=16,'col_0'=8,'col_1'=2] {'col_0','col_1'}, dimensions={0} | all-to-all | bytes 16384 | tf_op jit(solution)/shard_map/all_to_all | solution.py:13
  28.8 1.0 fusion.3
  29.8 0.2 broadcast_in_dim.9
  30.0 29.5 %all_to_all.17 = bf16[16,128,512]{2,1,0:T(8,128)(2,1)S(1)} all-to-all(bf16[16,128,512]{2,1,0:T(8,128)(2,1)S(1)} %broadcast_in_dim.9), channel_id=1, replica_groups=mesh['row'=16,'col_0'=8,'col_1'=2] {'row'}, dimensions={0} | all-to-all | bytes 4194304 | tf_op jit(solution)/shard_map/all_to_all | solution.py:13
  59.5 0.0 copy-done
  59.5 0.0 copy-start.1
  59.5 4.3 %convolution_convert_fusion = bf16[2048,1792]{0,1:T(8,128)(2,1)S(1)} fusion(bf16[2048,512]{1,0:T(8,128)(2,1)S(1)} %bitcast.10, bf16[512,1792]{1,0:T(8,128)(2,1)S(1)} %copy-done), kind=kOutput, calls=%fused_computation.1 | convolution fusion | flops 3761766400 | bytes 11272192 | tf_op jit(solution)/shard_map/dot_general | solution.py:69
  63.7 0.0 copy-done.1
  63.8 4.3 %convolution_convert_fusion.1 = bf16[2048,1792]{0,1:T(8,128)(2,1)S(1)} fusion(bf16[2048,512]{1,0:T(8,128)(2,1)S(1)} %bitcast.11, bf16[512,1792]{1,0:T(8,128)(2,1)S(1)} %copy-done.1), kind=kOutput, calls=%fused_computation.2 | convolution fusion | flops 3761766400 | bytes 11272192 | tf_op jit(solution)/shard_map/dot_general | solution.py:68
  68.0 17.1 %pad_maximum_fusion = bf16[2048,3584]{0,1:T(8,128)(2,1)} fusion(bf16[2048,1792]{0,1:T(8,128)(2,1)S(1)} %convolution_convert_fusion, bf16[2048,1792]{0,1:T(8,128)(2,1)S(1)} %convolution_convert_fusion.1), kind=kLoop, calls=%fused_computation | loop fusion | flops 29360128 | bytes 29360128 | tf_op jit(solution)/shard_map/concatenate | solution.py:70
  85.2 0.0 reduce-scatter.5.cloned.1.call-update
  85.2 0.0 reduce-scatter.7.cloned.1.call-start
  85.3 148.8 %reduce-scatter.5.cloned.1.call-done = bf16[256,3584]{0,1:T(8,128)(2,1)} async-done(((bf16[2048,3584]{0,1:T(8,128)(2,1)}), bf16[256,3584]{0,1:T(8,128)(2,1)}) %reduce-scatter.5.cloned.1.call-update) | async-done | bytes 1835024 | tf_op jit(solution)/shard_map/reduce_scatter | solution.py:34
  234.1 3.8 copy.7
  237.9 0.0 reduce-scatter.7.cloned.1.call-update
  237.9 0.0 all-gather.2.cloned.1.call-start
  238.0 34.4 %reduce-scatter.7.cloned.1.call-done = bf16[128,3584]{1,0:T(8,128)(2,1)} async-done(((bf16[256,3584]{1,0:T(8,128)(2,1)}), bf16[128,3584]{1,0:T(8,128)(2,1)}) %reduce-scatter.7.cloned.1.call-update) | async-done | bytes 917520
  272.3 1.5 copy.8
  273.9 0.1 convert_element_type.21
  274.0 0.2 fusion
  274.3 14.6 %all_gather.6 = bf16[256,1792]{0,1:T(8,128)(2,1)} all-gather(bf16[128,1792]{0,1:T(8,128)(2,1)S(1)} %fusion), channel_id=1, replica_groups=mesh['row'=16,'col_0'=8,'col_1'=2] {'col_1'}, dimensions={0}, use_global_device_ids=true | all-gather | bytes 1376256 | tf_op jit(solution)/shard_map/all_gather | solution.py:40
  288.9 0.0 all-gather.2.cloned.1.call-update
  288.9 88.7 %all-gather.2.cloned.1.call-done = bf16[2048,1792]{0,1:T(8,128)(2,1)} async-done(((bf16[256,1792]{0,1:T(8,128)(2,1)}), bf16[2048,1792]{0,1:T(8,128)(2,1)}) %all-gather.2.cloned.1.call-update) | async-done | bytes 7340048 | tf_op jit(solution)/shard_map/all_gather | solution.py:40
  377.6 7.6 %convolution_convert_fusion.2 = bf16[2048,512]{1,0:T(8,128)(2,1)S(1)} fusion(bf16[2048,1792]{0,1:T(8,128)(2,1)} %all-gather.2.cloned.1.call-done, bf16[1792,512]{1,0:T(8,128)(2,1)} %param.9), kind=kOutput, calls=%fused_computation.3 | convolution fusion | flops 3759144960 | bytes 11272192 | tf_op jit(solution)/shard_map/dot_general | solution.py:75
  385.2 30.4 %all_to_all.18 = bf16[16,128,512]{2,1,0:T(8,128)(2,1)} all-to-all(bf16[16,128,512]{2,1,0:T(8,128)(2,1)S(1)} %bitcast.12), channel_id=1, replica_groups=mesh['row'=16,'col_0'=8,'col_1'=2] {'row'}, dimensions={0} | all-to-all | bytes 4194304 | tf_op jit(solution)/shard_map/all_to_all | solution.py:52
  415.6 2.6 reduce_sum.32
  (3 shorter events, 0.0 us)
Async XLA Ops:
  6.5 52.9 %copy-start = (bf16[512,1792]{1,0:T(8,128)(2,1)S(1)}, bf16[512,1792]{1,0:T(8,128)(2,1)}, u32[]{:S(2)}) copy-start(bf16[512,1792]{1,0:T(8,128)(2,1)} %param.8) | copy-start | bytes 5505028
  6.5 227.5 %reduce-scatter.5.cloned.1.call-start = ((), (), s32[]{:S(2)}) async-start(), calls=%async_computation.5 | async-start | bytes 16515072 | tf_op jit(solution)/shard_map/reduce_scatter | solution.py:34
  59.5 4.3 %copy-start.1 = (bf16[512,1792]{1,0:T(8,128)(2,1)S(1)}, bf16[512,1792]{1,0:T(8,128)(2,1)}, u32[]{:S(2)}) copy-start(bf16[512,1792]{1,0:T(8,128)(2,1)} %param.7) | copy-start | bytes 5505028
  85.2 187.1 %reduce-scatter.7.cloned.1.call-start = ((), (), s32[]{:S(2)}) async-start(), calls=%async_computation.7 | async-start | bytes 2752512
  237.9 139.6 %all-gather.2.cloned.1.call-start = ((), (), s32[]{:S(2)}) async-start(), calls=%async_computation.6 | async-start | bytes 8257536 | tf_op jit(solution)/shard_map/all_gather | solution.py:40
Sparse Core Ops, SparseCore 0:
  85.3 148.7 reduce-scatter.4
  238.1 34.2 reduce-scatter.6
  289.0 88.5 all-gather.1
where the time goes:
time: 428 us; the launch traced here: 425 us
  waiting for transfers between devices  272 us (64%)
  blocking collectives  95.5 us (22%)
  other arithmetic  22.3 us (5%)
  matrix products  16.2 us (4%)
  between operations  13.2 us (3%)
  local copies, waits for them, and re-layouts  5.59 us (1%)
    reduce_scatter x1, waiting for transfers between devices, own_rows(): subtotal = lax.psum_scatter(subtotal, axis, scatter_dimension=0, tiled=True)  149 us
    all_gather x1, waiting for transfers between devices, gathered_by_axis(): shard = lax.all_gather(shard, axis, axis=dim, tiled=True)  88.7 us
    all_to_all x2, blocking collectives, from_everyone(): return lax.all_to_all(copies, axis, split_axis=0, concat_axis=0, tiled=True)  50.5 us
    unnamed x4, waiting for transfers between devices  34.4 us
    all_to_all x1, blocking collectives, sent_and_summed(): lax.all_to_all(in_blocks(shard, dim, count), axis, 0, 0, tiled=True)  30.4 us
    concatenate x1, other arithmetic, body(): sums = own_rows(jnp.concatenate([gate_term, up_term], axis=1), COL)  17.1 us
    all_gather x1, blocking collectives, gathered_by_axis(): shard = lax.all_gather(shard, axis, axis=dim, tiled=True)  14.6 us
  transfers between devices with their start and end apart: 3, of which 3 were waited for; matrix products, arithmetic and copies ran while one was open for 0% of the time, Pallas kernels for 0%

commit v1 on v0

v1 whole, which is shorter than its diff:
```python
import functools

import jax
import jax.numpy as jnp
from jax import lax
from jax.experimental import pallas as pl
from jax.experimental.pallas import tpu as pltpu
from jax.sharding import Mesh
from jax.sharding import PartitionSpec as P

MESH = pl.DeviceIdType.MESH
D = 8192
ROW = ("ylo", "x", "core")
COL = ("z", "yhi")
F32 = jnp.float32
BF16 = jnp.bfloat16
NZ = 8
NX = 4
NY = 4
PLANE = NX * NY
ROWS = 128
PIECE = ROWS // NZ
HALF = ROWS // 2
DS = 512
LANES = 128
NI = 7


def kernel(
    tok, gain, gate_w, up_w, down_w, out,
    X, Xg, W1, W2, R0, RS, H, O, OR, gsend, gbuf, sq, sqr, S,
    sem_g, sem_xy, sem_xx, sem_w, sem_wc, sem_w2, sem_sq, sem_rs, sem_ag, sem_o,
    snd_g, snd_xy, snd_xx, snd_xf, snd_w, snd_wc, snd_w2, snd_w2c, snd_sq, snd_rs, snd_ag, snd_agh, snd_o,
):
    ylo, x, core = (lax.axis_index(a) for a in ROW)
    z, yhi = (lax.axis_index(a) for a in COL)
    y = 2 * yhi + ylo
    mine = ylo * NX + x

    def remote(src, dst, send, recv, device):
        pltpu.make_async_remote_copy(
            src_ref=src, dst_ref=dst, send_sem=send, recv_sem=recv, device_id=device, device_id_type=MESH
        ).start()

    def arrived(ref, sem):
        pltpu.make_async_copy(ref, ref, sem).wait()

    def at_y(q):
        to = lax.rem(y + q, NY)
        return lax.rem(to, 2), to // 2

    def at_x(q):
        return lax.rem(x + q, NX)

    def at_z(q):
        return lax.rem(z + q + NZ, NZ)

    def in_plane(p):
        lo, hi = at_y(p // NX)
        return lo, hi, at_x(lax.rem(p, NX))

    barrier = pltpu.get_barrier_semaphore()

    @pl.loop(1, PLANE)
    def _(p):
        lo, hi, to_x = in_plane(p)
        pl.semaphore_signal(barrier, inc=1, device_id={"ylo": lo, "yhi": hi, "x": to_x}, device_id_type=MESH)

    @pl.loop(1, NZ)
    def _(p):
        pl.semaphore_signal(barrier, inc=1, device_id={"z": at_z(p)}, device_id_type=MESH)

    pl.semaphore_signal(barrier, inc=1, device_id={"core": 1 - core}, device_id_type=MESH)
    gsend[...] = jnp.broadcast_to(gain[...], gsend.shape)
    pl.semaphore_wait(barrier, PLANE - 1 + NZ - 1 + 1)

    def block_at(o):
        return at_z(lax.select(lax.rem(o, 2) == 1, (7 - o) // 2, 4 + o // 2))

    def own_piece(j):
        return tok.at[pl.ds(pl.multiple_of(j * PIECE, PIECE), PIECE)]

    def slot(j, row, half):
        return X.at[j, pl.ds(pl.multiple_of(row * PIECE, PIECE), PIECE), pl.ds(pl.multiple_of(half * DS, DS), DS)]

    @pl.loop(0, NZ)
    def _(o):
        j = block_at(o)
        for q in range(1, NY):
            lo, hi = at_y(q)
            remote(own_piece(j), slot(j, mine, yhi), snd_xy.at[q - 1], sem_xy.at[o], {"ylo": lo, "yhi": hi})

    for h in range(2):
        remote(gsend, gbuf.at[yhi], snd_g, sem_g, {"ylo": 1 - ylo, "yhi": h})

    half_width = NI * LANES

    @pl.loop(0, NI)
    def _(i):
        for h in range(2):
            columns = pl.ds(pl.multiple_of(h * half_width + i * LANES, LANES), LANES)
            rows = pl.ds(pl.multiple_of(yhi * DS, DS), DS)
            device = {"ylo": 1 - ylo, "yhi": h}
            remote(gate_w.at[:, columns], W1.at[i, core, rows, pl.ds(0, LANES)], snd_w, sem_w.at[i], device)
            remote(up_w.at[:, columns], W1.at[i, core, rows, pl.ds(LANES, LANES)], snd_w, sem_w.at[i], device)

    for h in range(2):
        remote(
            down_w.at[pl.ds(h * half_width, half_width)],
            W2.at[core, :, pl.ds(pl.multiple_of(yhi * DS, DS), DS)],
            snd_w2, sem_w2.at[0], {"ylo": 1 - ylo, "yhi": h},
        )

    @pl.loop(0, NZ)
    def _(o):
        j = block_at(o)
        for q in range(1, NX):
            remote(own_piece(j), slot(j, mine, yhi), snd_xx.at[q - 1], sem_xx.at[o], {"x": at_x(q)})
        X[j, pl.ds(pl.multiple_of(mine * PIECE, PIECE), PIECE), pl.ds(pl.multiple_of(yhi * DS, DS), DS)] = tok[
            pl.ds(pl.multiple_of(j * PIECE, PIECE), PIECE)
        ]
        arrived(X.at[0, pl.ds(0, 3 * PIECE), pl.ds(0, DS)], sem_xy.at[o])
        for r in range(1, NY):
            lo, hi = at_y(r)
            for q in range(1, NX):
                ref = slot(j, lo * NX + x, hi)
                remote(ref, ref, snd_xf.at[r - 1, q - 1], sem_xx.at[o], {"x": at_x(q)})

    arrived(gbuf, sem_g)

    def prepare(o):
        j = block_at(o)
        arrived(X.at[0, pl.ds(0, 6 * PIECE)], sem_xx.at[o])
        values = X[j].astype(F32)
        parts = [values[:, k * LANES : (k + 1) * LANES] for k in range(2 * DS // LANES)]
        total = functools.reduce(jnp.add, [part * part for part in parts])
        sq[j] = jnp.broadcast_to(jnp.sum(total.T, axis=0, keepdims=True), (8, LANES))
        for h in range(2):
            Xg[j, :, h * DS : (h + 1) * DS] = (values[:, h * DS : (h + 1) * DS] * gbuf[h, 0:1, :]).astype(BF16)
        return j

    def prepare_and_send(o):
        j = prepare(o)
        p = lax.rem(j - z + NZ, NZ)
        remote(sq.at[j], sqr.at[p], snd_sq, sem_sq, {"z": j})

    def product(j, i, k):
        return jnp.dot(Xg[j], W1[i, k], preferred_element_type=F32)

    signs = (1, -1)
    halves = (pl.ds(0, HALF), pl.ds(HALF, HALF))

    def columns_of(i, k):
        return pl.ds(pl.multiple_of((k * NI + i) * LANES, LANES), LANES)

    def finish(i, k):
        for d in range(2):
            arrived(RS.at[d, 3, i, k], sem_rs.at[d, 3, i, k])
        sums = product(z, i, k) + RS[0, 3, i, k].astype(F32) + RS[1, 3, i, k].astype(F32)
        gate = sums[:, :LANES] * S[...]
        up = sums[:, LANES:] * S[...]
        columns = columns_of(i, k)
        H[z, :, columns] = (gate / (1.0 + jnp.exp(-gate)) * up).astype(BF16)
        ref = H.at[z, :, columns]
        for d in range(2):
            remote(ref, ref, snd_ag.at[d, 0], sem_ag.at[d, 0, i, k], {"z": at_z(signs[d])})

    def pass_on(s, i, k):
        for d in range(2):
            j = at_z(signs[d] * (4 - s))
            ref = RS.at[d, s - 1, i, k]
            p = product(j, i, k)
            if s == 1:
                arrived(ref.at[halves[d]], sem_rs.at[d, 0, i, k])
                other = halves[1 - d]
                a, b = d * HALF, (1 - d) * HALF
                RS[d, 0, i, k, halves[d]] = (p[a : a + HALF] + RS[d, 0, i, k, halves[d]].astype(F32)).astype(BF16)
                RS[d, 0, i, k, other] = p[b : b + HALF].astype(BF16)
            else:
                arrived(ref, sem_rs.at[d, s - 1, i, k])
                RS[d, s - 1, i, k] = (p + RS[d, s - 1, i, k].astype(F32)).astype(BF16)
            remote(ref, RS.at[d, s, i, k], snd_rs.at[d, s], sem_rs.at[d, s, i, k], {"z": at_z(signs[d])})

    def open_up(i, k):
        R0[i, k] = product(at_z(4), i, k).astype(BF16)
        for d in range(2):
            remote(
                R0.at[i, k, halves[d]], RS.at[d, 0, i, k, halves[d]],
                snd_rs.at[d, 0], sem_rs.at[d, 0, i, k], {"z": at_z(signs[d])},
            )

    def pair_of_cores(c):
        return lax.rem(core + c, 2)

    @pl.loop(0, NI + 4)
    def _(w):
        @pl.when(w == 0)
        def _():
            prepare_and_send(0)

        @pl.when((w >= 1) & (w <= 3))
        def _():
            @pl.loop(0, 2)
            def _(c):
                prepare_and_send(2 * w - 1 + c)

        @pl.when(w == 4)
        def _():
            prepare(7)
            arrived(sqr.at[pl.ds(1, NZ - 1)], sem_sq)
            total = sq[z] + functools.reduce(jnp.add, [sqr[p] for p in range(1, NZ)])
            scale = lax.rsqrt(total[0:1] / D + 1e-05)
            S[...] = jnp.broadcast_to(scale, (LANES, LANES)).T

        @pl.when(w >= 4)
        def _():
            @pl.loop(0, 2)
            def _(c):
                finish(w - 4, pair_of_cores(c))

        for s in (3, 2, 1):
            @pl.when((w >= s) & (w - s < NI))
            def _(s=s):
                @pl.loop(0, 2)
                def _(c):
                    pass_on(s, w - s, pair_of_cores(c))

        @pl.when(w < NI)
        def _():
            arrived(W1.at[w, core], sem_w.at[w])
            remote(W1.at[w, core], W1.at[w, core], snd_wc, sem_wc.at[w], {"core": 1 - core})
            open_up(w, core)
            arrived(W1.at[w, 1 - core], sem_wc.at[w])
            open_up(w, 1 - core)

    arrived(W2.at[core], sem_w2.at[0])
    remote(W2.at[core], W2.at[core], snd_w2c, sem_w2.at[1], {"core": 1 - core})

    def mix(j):
        total = jnp.dot(H[j, :, :half_width], W2[0], preferred_element_type=F32)
        total = total + jnp.dot(H[j, :, half_width:], W2[1], preferred_element_type=F32)
        O[j] = total.astype(BF16)

        @pl.loop(1, PLANE)
        def _(p):
            lo, hi, to_x = in_plane(p)
            row = pl.ds(pl.multiple_of((lo * NX + to_x) * PIECE, PIECE), PIECE)
            column = pl.ds(pl.multiple_of(hi * DS, DS), DS)
            remote(O.at[j, row, column], OR.at[j, p], snd_o, sem_o.at[j], {"ylo": lo, "yhi": hi, "x": to_x})

    def forward(a, i, k):
        columns = columns_of(i, k)
        for d in range(2):
            j = at_z(-signs[d] * a)
            whole = H.at[j, :, columns]
            arrived(whole, sem_ag.at[d, a - 1, i, k])
            if a < 3:
                remote(whole, whole, snd_ag.at[d, a], sem_ag.at[d, a, i, k], {"z": at_z(signs[d])})
            else:
                part = H.at[j, halves[d], columns]
                remote(part, part, snd_agh.at[d], sem_ag.at[d, a, i, k], {"z": at_z(signs[d])})

    for a in range(1, 4):
        @pl.loop(0, 2)
        def _(h, a=a):
            k = pair_of_cores(h)

            if a == 1:
                @pl.loop(0, NI)
                def _(i):
                    forward(a, i, k)

                @pl.when(h == 0)
                def _():
                    arrived(W2.at[1 - core], sem_w2.at[1])
                    mix(z)
            else:
                mix(at_z((1 - 2 * h) * (a - 1)))

                @pl.loop(0, NI)
                def _(i):
                    forward(a, i, k)

    @pl.loop(0, 2)
    def _(h):
        mix(at_z((1 - 2 * h) * 3))

    far = at_z(4)

    @pl.loop(0, NI)
    def _(i):
        for k in range(2):
            for d in range(2):
                arrived(H.at[far, halves[d], columns_of(i, k)], sem_ag.at[d, 3, i, k])

    mix(far)

    @pl.loop(0, NZ)
    def _(o):
        j = block_at(7 - o)
        arrived(OR.at[j, pl.ds(1, PLANE - 1)], sem_o.at[j])
        own = O[j, pl.ds(pl.multiple_of(mine * PIECE, PIECE), PIECE), pl.ds(pl.multiple_of(yhi * DS, DS), DS)]
        total = own.astype(F32) + functools.reduce(jnp.add, [OR[j, p].astype(F32) for p in range(1, PLANE)])
        out[pl.ds(pl.multiple_of(j * PIECE, PIECE), PIECE)] = total.astype(BF16)

    arrived(gbuf, snd_g)
    for q in range(3):
        arrived(tok, snd_xy.at[q])
        arrived(tok, snd_xx.at[q])
        for r in range(3):
            arrived(tok, snd_xf.at[r, q])
    arrived(W1.at[:, 0], snd_w)
    arrived(W1.at[:, 0], snd_wc)
    arrived(W2.at[0], snd_w2)
    arrived(W2.at[0], snd_w2c)
    arrived(sqr.at[pl.ds(1, NZ - 1)], snd_sq)
    for d in range(2):
        arrived(R0.at[:, :, halves[d]], snd_rs.at[d, 0])
        for s in range(1, 4):
            arrived(RS.at[d, s], snd_rs.at[d, s])
        for a in range(3):
            arrived(H.at[0], snd_ag.at[d, a])
        arrived(H.at[0, halves[d]], snd_agh.at[d])
    arrived(OR.at[:, pl.ds(1, PLANE - 1)], snd_o)


def body(tokens, norm_gain, gate_weight, up_weight, down_weight):
    vmem = pl.BlockSpec(memory_space=pltpu.VMEM)
    hbm = pl.BlockSpec(memory_space=pl.ANY)
    dma = pltpu.SemaphoreType.DMA
    return pl.pallas_call(
        kernel,
        name="swiglu",
        out_shape=jax.ShapeDtypeStruct(tokens.shape, tokens.dtype),
        in_specs=[vmem, vmem, hbm, hbm, hbm],
        out_specs=vmem,
        scratch_shapes=[
            pltpu.VMEM((NZ, ROWS, 2 * DS), BF16),
            pltpu.VMEM((NZ, ROWS, 2 * DS), BF16),
            pltpu.VMEM((NI, 2, 2 * DS, 2 * LANES), BF16),
            pltpu.VMEM((2, NI * LANES, 2 * DS), BF16),
            pltpu.VMEM((NI, 2, ROWS, 2 * LANES), BF16),
            pltpu.VMEM((2, 4, NI, 2, ROWS, 2 * LANES), BF16),
            pltpu.VMEM((NZ, ROWS, 2 * NI * LANES), BF16),
            pltpu.VMEM((NZ, ROWS, 2 * DS), BF16),
            pltpu.VMEM((NZ, PLANE, PIECE, DS), BF16),
            pltpu.VMEM((8, DS), F32),
            pltpu.VMEM((2, 8, DS), F32),
            pltpu.VMEM((NZ, 8, LANES), F32),
            pltpu.VMEM((NZ, 8, LANES), F32),
            pltpu.VMEM((LANES, LANES), F32),
            dma, dma((NZ,)), dma((NZ,)), dma((NI,)), dma((NI,)), dma((2,)), dma,
            dma((2, 4, NI, 2)), dma((2, 4, NI, 2)), dma((NZ,)),
            dma, dma((3,)), dma((3,)), dma((3, 3)), dma, dma, dma, dma, dma,
            dma((2, 4)), dma((2, 3)), dma((2,)), dma,
        ],
        compiler_params=pltpu.CompilerParams(
            collective_id=0, has_side_effects=True, vmem_limit_bytes=60 * 1024 * 1024
        ),
    )(tokens, norm_gain.reshape(1, -1), gate_weight, up_weight, down_weight)


def solution(mesh):
    torus = Mesh(mesh.devices.reshape(2, NX, 2, NZ, 2), ROW + COL)
    return jax.shard_map(
        body,
        mesh=torus,
        in_specs=(P(ROW, COL), P(COL), P(COL, ROW), P(COL, ROW), P(ROW, COL)),
        out_specs=P(ROW, COL),
        check_vma=False,
    )
```

time: 428 us -> 148 us (0.35)
  waiting for transfers between devices: 272 us -> 0 us
  Pallas kernels: 0 us -> 146 us
  blocking collectives: 95.5 us -> 0 us
  other arithmetic: 22.3 us -> 0 us
  matrix products: 16.2 us -> 0 us
  between operations: 13.2 us -> 0.01 us
    reduce_scatter x1 -> x0, waiting for transfers between devices: 149 us -> none  [own_rows(): subtotal = lax.psum_scatter(subtotal, axis, scatter_dimension=0, tiled=True)]
    pallas_call x0 -> x1, Pallas kernels: none -> 146 us  [body(): pl.pallas_call(kernel, name='swiglu', out_shape=jax.ShapeDtypeStruct(toke...]
    all_gather x1 -> x0, waiting for transfers between devices: 88.7 us -> none  [gathered_by_axis(): shard = lax.all_gather(shard, axis, axis=dim, tiled=True)]
    all_to_all x3 -> x0, blocking collectives: 80.9 us -> none  [the longest x2 50.5 us: from_everyone(): return lax.all_to_all(copies, axis, split_axis=0, concat_axis=0, tiled=True)]
    unnamed x4 -> x0, waiting for transfers between devices: 34.4 us -> none
    concatenate x1 -> x0, other arithmetic: 17.1 us -> none  [body(): sums = own_rows(jnp.concatenate([gate_term, up_term], axis=1), COL)]
    dot_general x3 -> x0, matrix products: 16.2 us -> none  [the longest x1 7.6 us: body(): jnp.dot(picked, down_weight, preferred_element_type=jnp.float32)]
    all_gather x1 -> x0, blocking collectives: 14.6 us -> none  [gathered_by_axis(): shard = lax.all_gather(shard, axis, axis=dim, tiled=True)]
  transfers between devices with their start and end apart: 3 -> 0, of which waited for: 3 -> 0; matrix products, arithmetic and copies ran while one was open for 0% -> 0% of each run, Pallas kernels for 0% -> 0%
where the time goes in v1:
time: 148 us; the launch traced here: 147 us
  Pallas kernels  146 us (99%)
  local copies, waits for them, and re-layouts  1.57 us (1%)
    pallas_call x1, Pallas kernels, body(): pl.pallas_call(kernel, name='swiglu', out_shape=jax.ShapeDtypeStruct(toke...  146 us

profile of v1, /device:TPU:6, one launch (start us, length us, event | category | flops | bytes accessed | tf_op | source)
XLA Modules:
  0.0 147.1 jit_solution(12916200582739203436)
XLA Ops:
  0.0 145.5 %swiglu.1 = bf16[128,512]{1,0:T(8,128)(2,1)} custom-call(bf16[128,512]{1,0:T(8,128)(2,1)} %tok.1, f32[1,512]{1,0:T(1,128)} %bitcast.1, bf16[512,1792]{1,0:T(8,128)(2,1)} %gate_w.1, bf16[512,1792]{1,0:T(8,128)(2,1)} %up_w.1, bf16[1792,512]{1,0:T(8,128)(2,1)} %down_w.1), custom_call_target="tpu_custom_call" | custom-call | tf_op jit(solution)/shard_map/swiglu/pallas_call | solution.py:331
  145.5 1.6 %copy.7 = bf16[128,512]{1,0:T(8,128)(2,1)} copy(bf16[128,512]{1,0:T(8,128)(2,1)} %swiglu.1) | data formatting | bytes 262144
